TPU v7x, 32 devices: a whole 2x2x4 slice. The times are simulated.
32 devices in a mesh: owner: 4 (over y, core), rows: 8 (over z, x).
Axes of the slice: x: 2, y: 2, z: 4, core: 2. Of those that a mesh axis runs over, the one named last changes fastest.
Arguments:
- w_down: float32 [16, 6400, 4096], P('owner', None, 'rows'), may hold values from -0.109375 to 0.109375
- avg_down: bfloat16 [16, 6400, 4096], P('owner', None, 'rows'), may hold values from -0.0390625 to 0.0390625
- router_weight: float32 [4096, 16], P('rows', 'owner'), may hold values from -0.09375 to 0.09375
- router_gain: float32 [4096], P('rows'), may hold values from 0.25 to 1.75
Outputs:
- serve_down: bfloat16 [16, 6400, 4096], P('owner', 'rows')
- scale_down: float32 [16, 6400], P('owner', 'rows')
- serve_router: bfloat16 [4096, 16], replicated
All inputs are finite; a program needn't handle non-finite values.
Results may differ from a plain program's by a relative error of at most 0.0085.
Values may be sent and summed in bfloat16 or wider, within the bound.
A program may use at most 256 MiB of HBM per device.

v0:
```python
import jax
import jax.numpy as jnp
from jax import lax
from jax.sharding import PartitionSpec as P


def local(w_down, avg_down, router_weight, router_gain):
    fresh_down = w_down + avg_down.astype(jnp.float32)
    total_down = lax.psum(
        jnp.sum(fresh_down * fresh_down, axis=2).astype(jnp.bfloat16), "rows"
    ).astype(jnp.float32)
    scale_down = jnp.sqrt(total_down)
    narrow_down = (fresh_down / jnp.expand_dims(scale_down, 2)).astype(jnp.bfloat16)
    serve_down = lax.all_to_all(narrow_down, "rows", split_axis=1, concat_axis=2, tiled=True)
    scale_down = lax.dynamic_slice_in_dim(
        scale_down, lax.axis_index("rows") * serve_down.shape[1], serve_down.shape[1], axis=1
    )
    part_router = (router_weight * router_gain[:, None]).astype(jnp.bfloat16)
    row_router = lax.all_gather(part_router, "rows", axis=0, tiled=True)
    serve_router = lax.all_gather(row_router, "owner", axis=1, tiled=True)
    return (serve_down, scale_down, serve_router)


def solution(mesh):
    return jax.shard_map(
        local,
        mesh=mesh,
        in_specs=(
            P("owner", None, "rows"),
            P("owner", None, "rows"),
            P("rows", "owner"),
            P("rows"),
        ),
        out_specs=(P("owner", "rows", None), P("owner", "rows"), P()),
        check_vma=False,
    )
```

profile of v0, /device:TPU:0, one launch (start us, length us, event | category | flops | bytes accessed | tf_op | source)
XLA Modules:
  0.0 826.9 jit_solution(7862156734528137198)
XLA Ops:
  0.6 24.2 %multiply_reduce_fusion = bf16[4,6400]{1,0:T(4,128)(2,1)S(1)} fusion(f32[4,6400,512]{2,1,0:T(8,128)} %param.4, bf16[4,6400,512]{2,1,0:T(8,128)(2,1)} %param.5), kind=kLoop, calls=%fused_computation.1 | loop fusion | flops 52403200 | bytes 78694400 | tf_op jit(solution)/shard_map/reduce_sum | solution.py:10
  24.9 0.9 copy.21
  25.8 83.5 %psum.7 = bf16[4,6400]{0,1:T(8,128)(2,1)} all-reduce(bf16[4,6400]{0,1:T(8,128)(2,1)S(1)} %copy.21), channel_id=1, replica_groups=mesh['owner'=4,'rows'=8] {'rows'}, use_global_device_ids=true, to_apply=%region_1.0 | all-reduce | flops 25600 | bytes 102400 | tf_op jit(solution)/shard_map/psum | solution.py:9
  109.3 2.3 convert_sqrt_fusion
  111.6 1.2 copy.17
  112.8 34.3 %divide_convert_fusion = bf16[4,6400,512]{2,1,0:T(8,128)(2,1)} fusion(f32[4,6400,512]{2,1,0:T(8,128)} %param.4, bf16[4,6400,512]{2,1,0:T(8,128)(2,1)} %param.5, f32[4,6400]{1,0:T(4,128)S(1)} %copy.17), kind=kLoop, calls=%fused_computation | loop fusion | flops 52428800 | bytes 104960000 | tf_op jit(solution)/shard_map/convert_element_type | solution.py:13
  147.1 33.4 %copy.18 = bf16[4,6400,512]{2,0,1:T(4,128)(2,1)} copy(bf16[4,6400,512]{2,1,0:T(8,128)(2,1)} %divide_convert_fusion) | data formatting | bytes 52428800 | tf_op jit(solution)/shard_map/convert_element_type | solution.py:13
  180.5 0.0 copy-start
  180.5 0.0 copy-start.1
  180.5 6.6 all-to-all-start
  187.2 0.8 constant_dynamic-slice_fusion
  187.9 1.8 copy.20
  189.7 0.0 copy-done
  189.7 0.0 copy-done.1
  189.7 573.7 %all_gather.6 = bf16[4096,4]{0,1:T(4,128)(2,1)S(1)} all-gather(bf16[512,4]{0,1:T(4,128)(2,1)S(1)} %multiply_convert_fusion), channel_id=1, replica_groups=mesh['owner'=4,'rows'=8] {'rows'}, dimensions={0}, use_global_device_ids=true | all-gather | bytes 36864 | tf_op jit(solution)/shard_map/all_gather | solution.py:19
  763.4 5.4 all-gather
  768.8 0.7 reshape.9
  769.5 0.0 all-to-all-done
  769.5 18.2 %copy.19 = bf16[4,800,8,512]{3,2,1,0:T(8,128)(2,1)} copy(bf16[4,800,8,512]{3,0,1,2:T(4,128)(2,1)} %bitcast.1) | data formatting | bytes 52428800 | tf_op jit(solution)/shard_map/all_to_all | solution.py:14
  787.7 39.2 %all_to_all.16 = bf16[4,800,4096]{2,1,0:T(8,128)(2,1)} reshape(bf16[4,800,8,512]{3,2,1,0:T(8,128)(2,1)} %copy.19) | data formatting | bytes 52428800 | tf_op jit(solution)/shard_map/all_to_all | solution.py:14
  (1 shorter events, 0.0 us)
Async XLA Ops:
  180.5 9.2 %copy-start = (f32[512,4]{0,1:T(4,128)S(1)}, f32[512,4]{0,1:T(4,128)}, u32[]{:S(2)}) copy-start(f32[512,4]{0,1:T(4,128)} %param.6) | copy-start | bytes 24580
  180.5 9.2 %copy-start.1 = (f32[512]{0:T(512)S(1)}, f32[512]{0:T(512)}, u32[]{:S(2)}) copy-start(f32[512]{0:T(512)} %param.7) | copy-start | bytes 6148
  180.5 589.0 %all-to-all-start = ((bf16[4,6400,512]{2,0,1:T(4,128)(2,1)}), bf16[4,6400,512]{2,0,1:T(4,128)(2,1)}, u32[]{:S(2)}, u32[]{:S(2)}) async-start(bf16[4,6400,512]{2,0,1:T(4,128)(2,1)} %copy.18), calls=%async_computation | async-start | bytes 52428800 | tf_op jit(solution)/shard_map/all_to_all | solution.py:14
where the time goes:
time: 828 us; the launch traced here: 827 us
  blocking collectives  663 us (80%)
  local copies, waits for them, and re-layouts  96.2 us (12%)
  other arithmetic  60.8 us (7%)
    all_gather x1, blocking collectives, local(): row_router = lax.all_gather(part_router, 'rows', axis=0, tiled=True)  574 us
    psum x1, blocking collectives, local(): lax.psum(jnp.sum(fresh_down * fresh_down, axis=2).astype(jnp.bfloat16), '...  83.5 us
    all_to_all x2, local copies, waits for them, and re-layouts, local(): lax.all_to_all(narrow_down, 'rows', split_axis=1, concat_axis=2, tiled=True)  57.4 us
    convert_element_type x1, other arithmetic, local(): (fresh_down / jnp.expand_dims(scale_down, 2)).astype(jnp.bfloat16)  34.3 us
    convert_element_type x1, local copies, waits for them, and re-layouts, local(): (fresh_down / jnp.expand_dims(scale_down, 2)).astype(jnp.bfloat16)  33.4 us
    reduce_sum x1, other arithmetic, local(): jnp.sum(fresh_down * fresh_down, axis=2).astype(jnp.bfloat16)  24.2 us
  transfers between devices with their start and end apart: 1, of which 0 were waited for; matrix products, arithmetic and copies ran while one was open for 0% of the time, Pallas kernels for 0%

commit v1 on v0

--- a/solution.py
+++ b/solution.py
@@ -2,6 +2,17 @@
 import jax.numpy as jnp
 from jax import lax
 from jax.sharding import PartitionSpec as P
+
+
+def save_the_sums_all(mat, array_dim, state):
+    right_arr, moved = (mat.shape[:array_dim], mat.shape[array_dim + 1 :])
+    return jnp.moveaxis(mat.reshape(*right_arr, state, -1, *moved), array_dim, 0)
+
+
+def try_all_blocks_up(unit, row_dim):
+    response = list(unit.shape[1:])
+    response[row_dim] *= unit.shape[0]
+    return jnp.moveaxis(unit, 0, row_dim).reshape(response)
 
 
 def local(w_down, avg_down, router_weight, router_gain):
@@ -11,7 +22,18 @@
     ).astype(jnp.float32)
     scale_down = jnp.sqrt(total_down)
     narrow_down = (fresh_down / jnp.expand_dims(scale_down, 2)).astype(jnp.bfloat16)
-    serve_down = lax.all_to_all(narrow_down, "rows", split_axis=1, concat_axis=2, tiled=True)
+    opened, small = (lax.axis_size("rows"), lax.axis_index("rows"))
+    reply = save_the_sums_all(narrow_down, 1, opened)
+    wide_out = reply
+    for it in range(1, opened):
+        part_next, mid_arr = ((small + it) % opened, (small - it) % opened)
+        then = lax.dynamic_index_in_dim(reply, part_next, 0)
+        seen = []
+        for no in range(opened):
+            seen.append((no, (no + it) % opened))
+        spare = lax.ppermute(then, "rows", perm=seen)
+        wide_out = lax.dynamic_update_slice_in_dim(wide_out, spare, mid_arr, axis=0)
+    serve_down = try_all_blocks_up(wide_out, 2)
     scale_down = lax.dynamic_slice_in_dim(
         scale_down, lax.axis_index("rows") * serve_down.shape[1], serve_down.shape[1], axis=1
     )

time: 828 us -> 741 us (0.89)
  blocking collectives: 663 us -> 475 us
  waiting for transfers between devices: 0.01 us -> 71.6 us
  starting transfers between devices: 6.64 us -> 74.9 us
  local copies, waits for them, and re-layouts: 96.2 us -> 59.4 us
    all_gather x1, blocking collectives: 574 us -> 430 us  [local(): row_router = lax.all_gather(part_router, 'rows', axis=0, tiled=True)]
    ppermute x0 -> x7, starting transfers between devices: none -> 74.9 us  [local(): spare = lax.ppermute(then, 'rows', perm=seen)]
    ppermute x0 -> x7, waiting for transfers between devices: none -> 71.6 us  [local(): spare = lax.ppermute(then, 'rows', perm=seen)]
    all_to_all x2 -> x0, local copies, waits for them, and re-layouts: 57.4 us -> none  [local(): lax.all_to_all(narrow_down, 'rows', split_axis=1, concat_axis=2, tiled=True)]
    psum x1, blocking collectives: 83.5 us -> 39.3 us  [local(): lax.psum(jnp.sum(fresh_down * fresh_down, axis=2).astype(jnp.bfloat16), '...]
    convert_element_type x1 -> x0, local copies, waits for them, and re-layouts: 33.4 us -> none  [local(): (fresh_down / jnp.expand_dims(scale_down, 2)).astype(jnp.bfloat16)]
    dynamic_update_slice x0 -> x7, local copies, waits for them, and re-layouts: none -> 25.3 us  [local(): wide_out = lax.dynamic_update_slice_in_dim(wide_out, spare, mid_arr, axis=0)]
    reshape x0 -> x1, local copies, waits for them, and re-layouts: none -> 17.9 us  [try_all_blocks_up(): return jnp.moveaxis(unit, 0, row_dim).reshape(response)]
  transfers between devices with their start and end apart: 1 -> 7, of which waited for: 0 -> 1; matrix products, arithmetic and copies ran while one was open for 0% -> 3% of each run, Pallas kernels for 0% -> 0%
where the time goes in v1:
time: 741 us; the launch traced here: 740 us
  blocking collectives  475 us (64%)
  starting transfers between devices  74.9 us (10%)
  waiting for transfers between devices  71.6 us (10%)
  local copies, waits for them, and re-layouts  59.4 us (8%)
  other arithmetic  58.6 us (8%)
    all_gather x1, blocking collectives, local(): row_router = lax.all_gather(part_router, 'rows', axis=0, tiled=True)  430 us
    ppermute x7, starting transfers between devices, local(): spare = lax.ppermute(then, 'rows', perm=seen)  74.9 us
    ppermute x7, waiting for transfers between devices, local(): spare = lax.ppermute(then, 'rows', perm=seen)  71.6 us
    psum x1, blocking collectives, local(): lax.psum(jnp.sum(fresh_down * fresh_down, axis=2).astype(jnp.bfloat16), '...  39.3 us
    convert_element_type x1, other arithmetic, local(): (fresh_down / jnp.expand_dims(scale_down, 2)).astype(jnp.bfloat16)  34.3 us
    dynamic_update_slice x7, local copies, waits for them, and re-layouts, local(): wide_out = lax.dynamic_update_slice_in_dim(wide_out, spare, mid_arr, axis=0)  25.3 us
    reduce_sum x1, other arithmetic, local(): jnp.sum(fresh_down * fresh_down, axis=2).astype(jnp.bfloat16)  24.2 us
    reshape x1, local copies, waits for them, and re-layouts, try_all_blocks_up(): return jnp.moveaxis(unit, 0, row_dim).reshape(response)  17.9 us
  transfers between devices with their start and end apart: 7, of which 1 were waited for; matrix products, arithmetic and copies ran while one was open for 3% of the time, Pallas kernels for 0%

profile of v1, /device:TPU:0, one launch (start us, length us, event | category | flops | bytes accessed | tf_op | source)
XLA Modules:
  0.0 740.2 jit_solution(11643379839295329696)
XLA Ops:
  0.7 24.2 %multiply_reduce_fusion = bf16[4,6400]{1,0:T(4,128)(2,1)S(1)} fusion(f32[4,6400,512]{2,1,0:T(8,128)} %param.4, bf16[4,6400,512]{2,1,0:T(8,128)(2,1)} %param.5), kind=kLoop, calls=%fused_computation.1 | loop fusion | flops 52403200 | bytes 78694400 | tf_op jit(solution)/shard_map/reduce_sum | solution.py:21
  25.0 39.3 %psum.7 = bf16[4,6400]{1,0:T(4,128)(2,1)S(1)} all-reduce(bf16[4,6400]{1,0:T(4,128)(2,1)S(1)} %multiply_reduce_fusion), channel_id=1, replica_groups=mesh['owner'=4,'rows'=8] {'rows'}, use_global_device_ids=true, to_apply=%region_1.0 | all-reduce | flops 25600 | bytes 102400 | tf_op jit(solution)/shard_map/psum | solution.py:20
  64.3 0.1 convert_sqrt_fusion
  64.4 34.3 %divide_convert_fusion = bf16[4,6400,512]{2,1,0:T(8,128)(2,1)} fusion(f32[4,6400,512]{2,1,0:T(8,128)} %param.4, bf16[4,6400,512]{2,1,0:T(8,128)(2,1)} %param.5, f32[4,6400]{1,0:T(4,128)S(1)} %convert_sqrt_fusion), kind=kLoop, calls=%fused_computation | loop fusion | flops 52428800 | bytes 104960000 | tf_op jit(solution)/shard_map/convert_element_type | solution.py:24
  98.7 0.0 copy-start
  98.7 0.0 copy-start.1
  98.7 14.9 %dynamic-slice_bitcast_fusion = (bf16[1,4,800,512]{3,2,0,1:T(8,128)(2,1)}, bf16[1,4,800,512]{3,2,0,1:T(8,128)(2,1)}, bf16[1,4,800,512]{3,2,0,1:T(8,128)(2,1)}, b...) fusion(bf16[4,8,800,512]{3,2,1,0:T(8,128)(2,1)} %bitcast.38, ...), kind=kLoop, calls=%fused_computation.3 | loop fusion | bytes 45875228 | tf_op jit(solution)/shard_map/jit(dynamic_index_in_dim)/dynamic_slice | solution.py:30
  113.6 0.1 collective-permute-start
  113.7 0.1 collective-permute-start.1
  113.8 2.5 collective-permute-start.2
  116.2 2.7 collective-permute-start.3
  119.0 0.0 collective-permute-start.4
  119.0 71.6 %collective-permute-done = bf16[1,4,800,512]{3,2,0,1:T(8,128)(2,1)} collective-permute-done((bf16[1,4,800,512]{3,2,0,1:T(8,128)(2,1)}, bf16[1,4,800,512]{3,2,0,1:T(8,128)(2,1)}, u32[]{:S(2)}, u32[]{:S(2)}) %collective-permute-start) | collective-permute-done | bytes 3276832 | tf_op jit(solution)/shard_map/ppermute | solution.py:34
  190.6 0.0 collective-permute-start.5
  190.6 0.0 collective-permute-done.1
  190.6 69.5 %collective-permute-start.6 = (bf16[1,4,800,512]{3,2,0,1:T(8,128)(2,1)}, bf16[1,4,800,512]{3,2,0,1:T(8,128)(2,1)}, u32[]{:S(2)}, u32[]{:S(2)}) collective-permute-start(bf16[1,4,800,512]{3,2,0,1:T(8,128)(2,1)} %get-tuple-element.3), channel_id=1, source_target_pairs={{0,7},{1,0},{2,1},{3,2},{4,3},{5,4},{6,5},{7,6},{8,15},{9,8},{10,9... | collective-permute-start | bytes 9830408 | tf_op jit(solution)/shard_map/ppermute | solution.py:34
  260.1 0.0 copy-done
  260.1 0.0 copy-done.1
  260.1 430.1 %all_gather.6 = bf16[4096,4]{0,1:T(4,128)(2,1)S(1)} all-gather(bf16[512,4]{0,1:T(4,128)(2,1)S(1)} %multiply_convert_fusion), channel_id=1, replica_groups=mesh['owner'=4,'rows'=8] {'rows'}, dimensions={0}, use_global_device_ids=true | all-gather | bytes 36864 | tf_op jit(solution)/shard_map/all_gather | solution.py:41
  690.2 5.4 all-gather
  695.6 0.7 reshape.24
  696.3 0.7 constant_dynamic-slice_fusion
  697.0 3.9 constant_dynamic-update-slice_fusion.6
  700.9 4.0 constant_dynamic-update-slice_fusion.5
  704.8 0.0 collective-permute-done.2
  704.8 3.9 constant_dynamic-update-slice_fusion.4
  708.7 0.0 collective-permute-done.3
  708.7 3.8 constant_dynamic-update-slice_fusion.3
  712.5 0.0 collective-permute-done.4
  712.5 2.0 constant_dynamic-update-slice_fusion.2
  714.6 0.0 collective-permute-done.5
  714.6 3.9 constant_dynamic-update-slice_fusion.1
  718.4 0.0 collective-permute-done.6
  718.4 3.9 constant_dynamic-update-slice_fusion
  722.3 17.9 %copy.24 = bf16[4,8,100,8,512]{4,3,1,2,0:T(8,128)(2,1)} copy(bf16[4,8,100,8,512]{4,3,2,1,0:T(8,128)(2,1)} %bitcast.40) | data formatting | bytes 52428800 | tf_op jit(solution)/shard_map/reshape | solution.py:15
  (1 shorter events, 0.0 us)
Async XLA Ops:
  98.7 161.5 %copy-start = (f32[512,4]{0,1:T(4,128)S(1)}, f32[512,4]{0,1:T(4,128)}, u32[]{:S(2)}) copy-start(f32[512,4]{0,1:T(4,128)} %param.6) | copy-start | bytes 24580
  98.7 161.5 %copy-start.1 = (f32[512]{0:T(512)S(1)}, f32[512]{0:T(512)}, u32[]{:S(2)}) copy-start(f32[512]{0:T(512)} %param.7) | copy-start | bytes 6148
  113.6 77.0 %collective-permute-start = (bf16[1,4,800,512]{3,2,0,1:T(8,128)(2,1)}, bf16[1,4,800,512]{3,2,0,1:T(8,128)(2,1)}, u32[]{:S(2)}, u32[]{:S(2)}) collective-permute-start(bf16[1,4,800,512]{3,2,0,1:T(8,128)(2,1)} %get-tuple-element.9), channel_id=1, source_target_pairs={{0,1},{1,2},{2,3},{3,4},{4,5},{5,6},{6,7},{7,0},{8,9},{9,10},{10,1... | collective-permute-start | bytes 9830408 | tf_op jit(solution)/shard_map/ppermute | solution.py:34
  113.7 76.9 %collective-permute-start.1 = (bf16[1,4,800,512]{3,2,0,1:T(8,128)(2,1)S(1)}, bf16[1,4,800,512]{3,2,0,1:T(8,128)(2,1)}, u32[]{:S(2)}, u32[]{:S(2)}) collective-permute-start(bf16[1,4,800,512]{3,2,0,1:T(8,128)(2,1)S(1)} %get-tuple-element.8), channel_id=1, source_target_pairs={{0,2},{1,3},{2,4},{3,5},{4,6},{5,7},{6,0},{7,1},{8,10},{9,11},{10,... | collective-permute-start | bytes 9830408 | tf_op jit(solution)/shard_map/ppermute | solution.py:34
  113.8 591.1 %collective-permute-start.2 = (bf16[1,4,800,512]{3,2,0,1:T(8,128)(2,1)}, bf16[1,4,800,512]{3,2,0,1:T(8,128)(2,1)}, u32[]{:S(2)}, u32[]{:S(2)}) collective-permute-start(bf16[1,4,800,512]{3,2,0,1:T(8,128)(2,1)} %get-tuple-element.7), channel_id=1, source_target_pairs={{0,3},{1,4},{2,5},{3,6},{4,7},{5,0},{6,1},{7,2},{8,11},{9,12},{10,... | collective-permute-start | bytes 9830408 | tf_op jit(solution)/shard_map/ppermute | solution.py:34
  116.2 592.5 %collective-permute-start.3 = (bf16[1,4,800,512]{3,2,0,1:T(8,128)(2,1)}, bf16[1,4,800,512]{3,2,0,1:T(8,128)(2,1)}, u32[]{:S(2)}, u32[]{:S(2)}) collective-permute-start(bf16[1,4,800,512]{3,2,0,1:T(8,128)(2,1)} %get-tuple-element.6), channel_id=1, source_target_pairs={{0,4},{1,5},{2,6},{3,7},{4,0},{5,1},{6,2},{7,3},{8,12},{9,13},{10,... | collective-permute-start | bytes 9830408 | tf_op jit(solution)/shard_map/ppermute | solution.py:34
  119.0 593.6 %collective-permute-start.4 = (bf16[1,4,800,512]{3,2,0,1:T(8,128)(2,1)}, bf16[1,4,800,512]{3,2,0,1:T(8,128)(2,1)S(1)}, u32[]{:S(2)}, u32[]{:S(2)}) collective-permute-start(bf16[1,4,800,512]{3,2,0,1:T(8,128)(2,1)} %get-tuple-element.5), channel_id=1, source_target_pairs={{0,5},{1,6},{2,7},{3,0},{4,1},{5,2},{6,3},{7,4},{8,13},{9,14},{10,... | collective-permute-start | bytes 9830408 | tf_op jit(solution)/shard_map/ppermute | solution.py:34
  190.6 524.0 %collective-permute-start.5 = (bf16[1,4,800,512]{3,2,0,1:T(8,128)(2,1)}, bf16[1,4,800,512]{3,2,0,1:T(8,128)(2,1)}, u32[]{:S(2)}, u32[]{:S(2)}) collective-permute-start(bf16[1,4,800,512]{3,2,0,1:T(8,128)(2,1)} %get-tuple-element.4), channel_id=1, source_target_pairs={{0,6},{1,7},{2,0},{3,1},{4,2},{5,3},{6,4},{7,5},{8,14},{9,15},{10,... | collective-permute-start | bytes 9830408 | tf_op jit(solution)/shard_map/ppermute | solution.py:34
  190.6 527.9 %collective-permute-start.6 = (bf16[1,4,800,512]{3,2,0,1:T(8,128)(2,1)}, bf16[1,4,800,512]{3,2,0,1:T(8,128)(2,1)}, u32[]{:S(2)}, u32[]{:S(2)}) collective-permute-start(bf16[1,4,800,512]{3,2,0,1:T(8,128)(2,1)} %get-tuple-element.3), channel_id=1, source_target_pairs={{0,7},{1,0},{2,1},{3,2},{4,3},{5,4},{6,5},{7,6},{8,15},{9,8},{10,9... | collective-permute-start | bytes 9830408 | tf_op jit(solution)/shard_map/ppermute | solution.py:34
